TPU v7x, 32 devices: a whole 2x2x4 slice. The times are simulated.
32 devices in a mesh: data: 2 (over x), c: 4 (over z), r: 4 (over y, core).
Axes of the slice: x: 2, y: 2, z: 4, core: 2. Of those that a mesh axis runs over, the one named last changes fastest.
Arguments:
- x: bfloat16 [4096, 3584], P(('data', 'r'), 'c'), parts along dimension 0
- w: bfloat16 [3584, 28672], P('r', 'c')
- dy: bfloat16 [4096, 28672], P(('data', 'r'), 'c'), parts along dimension 0
Outputs:
- output 1: bfloat16 [4096, 3584], P(('data', 'r'), 'c'), parts along dimension 0
- output 2: float32 [7168, 28672], P(('data', 'r'), 'c'), parts along dimension 0
There are 2 independent parts. A program takes and returns all parts, laid end to end along the dimension named above; an argument that names none is the same for every part.
All inputs are finite; a program needn't handle non-finite values.
Results may differ from a plain program's by a relative error of at most 0.001.
Values are sent between devices in bfloat16 or wider.
A program may use at most 1 GiB of HBM per device.

v0:
```python
import jax
import jax.numpy as jnp
from jax import lax
from jax.sharding import PartitionSpec as P


def solution(mesh):
    rows = P(("data", "r"), "c")

    def local(x, w, dy):
        w_full_k = lax.all_gather(w, "r", axis=0, tiled=True)
        pdx = lax.dot_general(dy, w_full_k, (((1,), (1,)), ((), ())), preferred_element_type=jnp.float32)
        dx = lax.psum_scatter(pdx, "c", scatter_dimension=1, tiled=True).astype(jnp.bfloat16)
        x_full_k = lax.all_gather(x, "c", axis=1, tiled=True)
        pdw = lax.dot_general(x_full_k, dy, (((0,), (0,)), ((), ())), preferred_element_type=jnp.float32)
        dw = lax.psum_scatter(pdw, "r", scatter_dimension=0, tiled=True)
        return dx, dw

    return jax.shard_map(local, mesh=mesh, in_specs=(rows, P("r", "c"), rows), out_specs=(rows, rows), check_vma=False)
```

profile of v0, /device:TPU:0, one launch (start us, length us, event | category | flops | bytes accessed | tf_op | source)
XLA Modules:
  0.0 1187.7 jit_solution(2515362492062086544)
XLA Ops:
  7.2 0.0 all-gather.3.cloned.1.call-start
  7.2 0.7 all-gather.3.cloned.1.call-update
  7.9 0.0 all-gather.5.cloned.1.call-start
  7.9 0.7 all-gather.5.cloned.1.call-update
  8.6 0.0 reduce-scatter.3.cloned.1.call-start
  8.7 309.0 %all-gather.3.cloned.1.call-done = bf16[3584,7168]{1,0:T(8,128)(2,1)} async-done(((bf16[896,7168]{1,0:T(8,128)(2,1)}), bf16[3584,7168]{1,0:T(8,128)(2,1)}) %all-gather.3.cloned.1.call-update) | async-done | bytes 51380240 | tf_op jit(solution)/shard_map/all_gather | solution.py:11
  317.7 35.5 %fusion = f32[512,3584]{1,0:T(8,128)} fusion(bf16[512,7168]{1,0:T(8,128)(2,1)} %param.5, bf16[3584,7168]{1,0:T(8,128)(2,1)} %all-gather.3.cloned.1.call-done), kind=kOutput, calls=%fused_computation | convolution fusion | flops 26306674688 | bytes 66060288 | tf_op jit(solution)/shard_map/dot_general | solution.py:12
  353.2 0.0 reduce-scatter.3.cloned.1.call-update
  353.2 0.0 reduce-scatter.5.cloned.1.call-start
  353.3 37.5 %all-gather.5.cloned.1.call-done = bf16[512,3584]{1,0:T(8,128)(2,1)} async-done(((bf16[512,896]{1,0:T(8,128)(2,1)}), bf16[512,3584]{1,0:T(8,128)(2,1)}) %all-gather.5.cloned.1.call-update) | async-done | bytes 3670032 | tf_op jit(solution)/shard_map/all_gather | solution.py:14
  390.8 42.5 %fusion.1 = f32[3584,7168]{1,0:T(8,128)} fusion(bf16[512,3584]{1,0:T(8,128)(2,1)} %all-gather.5.cloned.1.call-done, bf16[512,7168]{1,0:T(8,128)(2,1)} %param.5), kind=kOutput, calls=%fused_computation.1 | convolution fusion | flops 26306674688 | bytes 113770496 | tf_op jit(solution)/shard_map/dot_general | solution.py:15
  433.3 0.0 reduce-scatter.5.cloned.1.call-update
  433.4 86.1 %reduce-scatter.3.cloned.1.call-done = f32[512,896]{1,0:T(8,128)} async-done(((f32[512,3584]{1,0:T(8,128)}), f32[512,896]{1,0:T(8,128)}) %reduce-scatter.3.cloned.1.call-update) | async-done | bytes 1835024 | tf_op jit(solution)/shard_map/reduce_scatter | solution.py:13
  519.5 2.5 convert_element_type.3
  522.0 659.2 %reduce-scatter.5.cloned.1.call-done = f32[896,7168]{1,0:T(8,128)} async-done(((f32[3584,7168]{1,0:T(8,128)}), f32[896,7168]{1,0:T(8,128)}) %reduce-scatter.5.cloned.1.call-update) | async-done | bytes 25690128 | tf_op jit(solution)/shard_map/reduce_scatter | solution.py:16
Async XLA Ops:
  7.2 310.5 %all-gather.3.cloned.1.call-start = ((), (), s32[]{:S(2)}) async-start(), calls=%async_computation.2 | async-start | bytes 64225280 | tf_op jit(solution)/shard_map/all_gather | solution.py:11
  7.9 382.9 %all-gather.5.cloned.1.call-start = ((), (), s32[]{:S(2)}) async-start(), calls=%async_computation.4 | async-start | bytes 4587520 | tf_op jit(solution)/shard_map/all_gather | solution.py:14
  8.6 510.8 %reduce-scatter.3.cloned.1.call-start = ((), (), s32[]{:S(2)}) async-start(), calls=%async_computation.3 | async-start | bytes 9175040 | tf_op jit(solution)/shard_map/reduce_scatter | solution.py:13
  353.2 827.9 %reduce-scatter.5.cloned.1.call-start = ((), (), s32[]{:S(2)}) async-start(), calls=%async_computation.5 | async-start | bytes 128450560 | tf_op jit(solution)/shard_map/reduce_scatter | solution.py:16
Sparse Core Ops, SparseCore 0:
  9.5 308.1 all-gather.2
  319.3 71.4 all-gather.4
  393.1 126.3 reduce-scatter.2
  522.5 658.5 reduce-scatter.4
where the time goes:
time: 1190 us
  waiting for transfers between devices  1090 us (92%)
  matrix products  78.1 us (7%)
  between operations  13.8 us (1%)
    reduce_scatter x1, waiting for transfers between devices, local(): dw = lax.psum_scatter(pdw, 'r', scatter_dimension=0, tiled=True)  659 us
    all_gather x1, waiting for transfers between devices, local(): w_full_k = lax.all_gather(w, 'r', axis=0, tiled=True)  309 us
    reduce_scatter x1, waiting for transfers between devices, local(): lax.psum_scatter(pdx, 'c', scatter_dimension=1, tiled=True)  86.1 us
    dot_general x1, matrix products, local(): lax.dot_general(x_full_k, dy, (((0,), (0,)), ((), ())), preferred_element...  42.5 us
    all_gather x1, waiting for transfers between devices, local(): x_full_k = lax.all_gather(x, 'c', axis=1, tiled=True)  37.5 us
    dot_general x1, matrix products, local(): lax.dot_general(dy, w_full_k, (((1,), (1,)), ((), ())), preferred_element...  35.5 us
  transfers between devices with their start and end apart: 4, of which 4 were waited for; matrix products, arithmetic and copies ran while one was open for 7% of the time, Pallas kernels for 0%

commit v1 on v0

v1 whole, which is shorter than its diff:
```python
import jax
import jax.numpy as jnp
from jax import lax
from jax.sharding import PartitionSpec as P


def solution(mesh):
    rows = P(("data", "r"), "c")
    n = mesh.shape["r"]
    swap = [(c * n + r, r * n + c) for c in range(n) for r in range(n)]

    def local(x, w, dy):
        dy_full = lax.all_gather(dy, "r", axis=0, tiled=True)
        x_swap = lax.ppermute(x, ("c", "r"), swap)
        x_full = lax.all_gather(x_swap, "c", axis=0, tiled=True)
        pdx = lax.dot_general(dy_full, w, (((1,), (1,)), ((), ())), preferred_element_type=jnp.float32)
        dx = lax.psum_scatter(pdx, "c", scatter_dimension=0, tiled=True).astype(jnp.bfloat16)
        dx = lax.ppermute(dx, ("c", "r"), swap)
        dw = lax.dot_general(x_full, dy_full, (((0,), (0,)), ((), ())), preferred_element_type=jnp.float32)
        return dx, dw

    return jax.shard_map(local, mesh=mesh, in_specs=(rows, P("r", "c"), rows), out_specs=(rows, rows), check_vma=False)
```

time: 1190 us -> 539 us (0.45)
  waiting for transfers between devices: 1090 us -> 447 us
    reduce_scatter x2 -> x1, waiting for transfers between devices: 745 us -> 152 us  [local(): lax.psum_scatter(pdx, 'c', scatter_dimension=0, tiled=True)]
    all_gather x2, waiting for transfers between devices: 346 us -> 294 us  [the longest x1 183 us: local(): dy_full = lax.all_gather(dy, 'r', axis=0, tiled=True)]
  transfers between devices with their start and end apart: 4 -> 5, of which waited for: 4 -> 3; matrix products, arithmetic and copies ran while one was open for 7% -> 7% of each run, Pallas kernels for 0% -> 0%
where the time goes in v1:
time: 539 us
  waiting for transfers between devices  447 us (83%)
  matrix products  72.5 us (13%)
  between operations  13.8 us (3%)
    all_gather x1, waiting for transfers between devices, local(): dy_full = lax.all_gather(dy, 'r', axis=0, tiled=True)  183 us
    reduce_scatter x1, waiting for transfers between devices, local(): lax.psum_scatter(pdx, 'c', scatter_dimension=0, tiled=True)  152 us
    all_gather x1, waiting for transfers between devices, local(): x_full = lax.all_gather(x_swap, 'c', axis=0, tiled=True)  111 us
    dot_general x1, matrix products, local(): lax.dot_general(dy_full, w, (((1,), (1,)), ((), ())), preferred_element_t...  37.9 us
    dot_general x1, matrix products, local(): lax.dot_general(x_full, dy_full, (((0,), (0,)), ((), ())), preferred_elem...  34.6 us
  transfers between devices with their start and end apart: 5, of which 3 were waited for; matrix products, arithmetic and copies ran while one was open for 7% of the time, Pallas kernels for 0%

profile of v1, /device:TPU:0, one launch (start us, length us, event | category | flops | bytes accessed | tf_op | source)
XLA Modules:
  0.0 538.7 jit_solution(1533198976574906745)
XLA Ops:
  7.2 0.0 all-gather.3.cloned.1.call-start
  7.2 0.7 all-gather.3.cloned.1.call-update
  7.9 0.0 copy-start.1
  7.9 0.0 reduce-scatter.2.cloned.1.call-start
  8.0 183.2 %all-gather.3.cloned.1.call-done = bf16[2048,7168]{1,0:T(8,128)(2,1)} async-done(((bf16[512,7168]{1,0:T(8,128)(2,1)}), bf16[2048,7168]{1,0:T(8,128)(2,1)}) %all-gather.3.cloned.1.call-update) | async-done | bytes 29360144 | tf_op jit(solution)/shard_map/all_gather | solution.py:13
  191.2 37.9 %fusion = f32[2048,896]{1,0:T(8,128)} fusion(bf16[2048,7168]{1,0:T(8,128)(2,1)} %all-gather.3.cloned.1.call-done, bf16[896,7168]{1,0:T(8,128)(2,1)} %param.4), kind=kOutput, calls=%fused_computation | convolution fusion | flops 26306674688 | bytes 49545216 | tf_op jit(solution)/shard_map/dot_general | solution.py:16
  229.1 0.0 reduce-scatter.2.cloned.1.call-update
  229.1 0.0 all-gather.5.cloned.1.call-start
  229.2 0.0 copy-done.1
  229.2 0.7 collective-permute-start.1
  229.9 0.0 collective-permute-done.1
  229.9 0.0 copy-start
  229.9 0.9 copy-done
  230.8 0.0 all-gather.5.cloned.1.call-update
  230.9 152.5 %reduce-scatter.2.cloned.1.call-done = f32[512,896]{1,0:T(8,128)} async-done(((f32[2048,896]{1,0:T(8,128)}), f32[512,896]{1,0:T(8,128)}) %reduce-scatter.2.cloned.1.call-update) | async-done | bytes 1835024 | tf_op jit(solution)/shard_map/reduce_scatter | solution.py:17
  383.4 1.6 convert_element_type.3
  384.9 0.7 collective-permute-start
  385.7 111.0 %all-gather.5.cloned.1.call-done = bf16[2048,896]{1,0:T(8,128)(2,1)} async-done(((bf16[512,896]{1,0:T(8,128)(2,1)}), bf16[2048,896]{1,0:T(8,128)(2,1)}) %all-gather.5.cloned.1.call-update) | async-done | bytes 3670032 | tf_op jit(solution)/shard_map/all_gather | solution.py:15
  496.7 34.6 %fusion.1 = f32[896,7168]{1,0:T(8,128)} fusion(bf16[2048,896]{1,0:T(8,128)(2,1)} %all-gather.5.cloned.1.call-done, bf16[2048,7168]{1,0:T(8,128)(2,1)} %all-gather.3.cloned.1.call-done), kind=kOutput, calls=%fused_computation.1 | convolution fusion | flops 26306674688 | bytes 58720256 | tf_op jit(solution)/shard_map/dot_general | solution.py:19
  531.3 0.0 collective-permute-done
  531.3 0.9 copy.6
Async XLA Ops:
  7.2 184.0 %all-gather.3.cloned.1.call-start = ((), (), s32[]{:S(2)}) async-start(), calls=%async_computation.1 | async-start | bytes 36700160 | tf_op jit(solution)/shard_map/all_gather | solution.py:13
  7.9 221.3 %copy-start.1 = (bf16[512,896]{1,0:T(8,128)(2,1)S(1)}, bf16[512,896]{1,0:T(8,128)(2,1)}, u32[]{:S(2)}) copy-start(bf16[512,896]{1,0:T(8,128)(2,1)} %param.3) | copy-start | bytes 2752516
  7.9 375.4 %reduce-scatter.2.cloned.1.call-start = ((), (), s32[]{:S(2)}) async-start(), calls=%async_computation.2 | async-start | bytes 9175040 | tf_op jit(solution)/shard_map/reduce_scatter | solution.py:17
  229.1 267.6 %all-gather.5.cloned.1.call-start = ((), (), s32[]{:S(2)}) async-start(), calls=%async_computation.3 | async-start | bytes 4587520 | tf_op jit(solution)/shard_map/all_gather | solution.py:15
  229.2 0.7 collective-permute-start.1
  229.9 0.9 copy-start
  384.9 146.3 %collective-permute-start = (bf16[512,896]{1,0:T(8,128)(2,1)S(1)}, bf16[512,896]{1,0:T(8,128)(2,1)S(1)}, u32[]{:S(2)}, u32[]{:S(2)}) collective-permute-start(bf16[512,896]{1,0:T(8,128)(2,1)S(1)} %convert_element_type.3), channel_id=1, source_target_pairs={{0,0},{1,4},{2,8},{3,12},{4,1},{5,5},{6,9},{7,13},{8,2},{9,6},{10,... | collective-permute-start | bytes 2752520 | tf_op jit(solution)/shard_map/ppermute | solution.py:18
Sparse Core Ops, SparseCore 0:
  9.5 181.5 all-gather.2
  229.2 154.0 reduce-scatter.1
  385.5 111.1 all-gather.4

commit v2 on v0

v2 whole, which is shorter than its diff:
```python
import jax
import jax.numpy as jnp
from jax import lax
from jax.experimental import pallas as pl
from jax.experimental.pallas import tpu as pltpu
from jax.sharding import PartitionSpec as P

MESH = pl.DeviceIdType.MESH
PIECES = 4
STEPS = 2 * PIECES
SLOTS = 4


def pick(size, want):
    return want if size % want == 0 else 128


def kernel(
    x_ref, w_ref, dy_ref, dx_ref, dw_ref,
    dyf, wv, xf, pbuf, rb1, rb2, fbuf, obuf,
    ld_sem, w_sem, y_send, y_recv, d_send, d_recv, e_send, e_recv,
    z1_send, z1_recv, z2_send, z2_recv, f_send, f_recv,
    x_src, x_recv, x_left, x_right, o_sem,
):
    z, r = lax.axis_index("c"), lax.axis_index("r")
    y, k = r // 2, r % 2
    mate, over, over_mate = 2 * y + 1 - k, 2 * (1 - y) + k, 2 * (1 - y) + 1 - k
    zb, zh = z % 2, z // 2
    z1, z2 = 2 * zh + 1 - zb, 2 * (1 - zh) + zb
    tb, kb = x_ref.shape
    nb = dy_ref.shape[1]
    pr = tb // PIECES
    sub = pr // 2
    kc, nc = pick(nb, 1024), pick(nb, 512)

    def rows(block, p):
        return pl.ds(pl.multiple_of(block * tb + p * pr, pr), pr)

    def send(src, dst, ssem, rsem, c=None, rr=None):
        dev = {}
        if c is not None:
            dev["c"] = c
        if rr is not None:
            dev["r"] = rr
        return pltpu.make_async_remote_copy(
            src_ref=src, dst_ref=dst, send_sem=ssem, recv_sem=rsem, device_id=dev, device_id_type=MESH
        )

    def load(p):
        return pltpu.make_async_copy(dy_ref.at[pl.ds(p * pr, pr)], dyf.at[rows(r, p)], ld_sem.at[p])

    w_load = pltpu.make_async_copy(w_ref, wv, w_sem)
    for p in range(PIECES):
        load(p).start()
    w_load.start()

    barrier = pltpu.get_barrier_semaphore()
    for i in range(1, 16):
        peer = {"c": (z + i // 4) % 4, "r": (r + i % 4) % 4}
        pl.semaphore_signal(barrier, inc=1, device_id=peer, device_id_type=MESH)
    pl.semaphore_wait(barrier, 15)

    def xrows(t):
        return pl.ds(pl.multiple_of(t * tb, tb), tb)

    x_own = pltpu.make_async_copy(x_ref, xf.at[xrows(r)], x_recv.at[r])
    x_out = send(x_ref, xf.at[xrows(r)], x_src.at[0], x_recv.at[r], c=z, rr=z)

    @pl.when(r == z)
    def _():
        x_own.start()

    @pl.when(r != z)
    def _():
        x_out.start()

    def y_copy(p):
        return send(dyf.at[rows(r, p)], dyf.at[rows(r, p)], y_send.at[p], y_recv.at[p], rr=over)

    def d_copy(p):
        return send(dyf.at[rows(r, p)], dyf.at[rows(r, p)], d_send.at[p], d_recv.at[p], rr=mate)

    def e_copy(p):
        return send(dyf.at[rows(over, p)], dyf.at[rows(over, p)], e_send.at[p], e_recv.at[p], rr=mate)

    def y_arrival(p):
        return send(dyf.at[rows(over, p)], dyf.at[rows(over, p)], y_send.at[p], y_recv.at[p], rr=over)

    def d_arrival(p):
        return send(dyf.at[rows(mate, p)], dyf.at[rows(mate, p)], d_send.at[p], d_recv.at[p], rr=mate)

    def e_arrival(p):
        return send(dyf.at[rows(over_mate, p)], dyf.at[rows(over_mate, p)], e_send.at[p], e_recv.at[p], rr=mate)

    for p in range(PIECES):
        load(p).wait()
        y_copy(p).start()
        d_copy(p).start()

    dist = jnp.where(z >= r, z - r, r - z)

    def x_right_copy(t):
        return send(xf.at[xrows(t)], xf.at[xrows(t)], x_right.at[t], x_recv.at[t], c=z + 1)

    def x_left_copy(t):
        return send(xf.at[xrows(t)], xf.at[xrows(t)], x_left.at[t], x_recv.at[t], c=z - 1)

    go_right = jnp.logical_and(z >= r, z < 3)
    go_left = jnp.logical_and(z <= r, z > 0)

    def x_point(j):
        t = j - dist
        live = jnp.logical_and(t >= 0, t < 4)

        @pl.when(live)
        def _():
            pltpu.make_async_copy(x_ref, xf.at[xrows(t)], x_recv.at[t]).wait()

        @pl.when(jnp.logical_and(live, go_right))
        def _():
            x_right_copy(t).start()

        @pl.when(jnp.logical_and(live, go_left))
        def _():
            x_left_copy(t).start()

    def blocks(s):
        return (r, mate, s) if s < PIECES else (over, over_mate, s - PIECES)

    def z1_copy(s):
        half = pl.ds(pl.multiple_of((1 - zb) * pr, pr), pr)
        return send(pbuf.at[s % SLOTS, half], rb1.at[s], z1_send.at[s], z1_recv.at[s], c=z1)

    def kept(i):
        return pl.ds(pl.multiple_of(zb * pr + i * sub, sub), sub)

    def part(i):
        return pl.ds(pl.multiple_of(i * sub, sub), sub)

    def z2_copy(s):
        return send(pbuf.at[s % SLOTS, kept(1 - zh)], rb2.at[s], z2_send.at[s], z2_recv.at[s], c=z2)

    def f_start(s, begin):
        a, b, p = blocks(s)
        owner = a + zb * (b - a)
        dst = dx_ref.at[pl.ds(pl.multiple_of(p * pr + zh * sub, sub), sub)]
        away = jnp.logical_or(z != r, owner != r)

        @pl.when(away)
        def _():
            copy = send(fbuf.at[s], dst, f_send.at[s], f_recv.at[0], c=r, rr=owner)
            copy.start() if begin else copy.wait_send()

        if begin:

            @pl.when(jnp.logical_not(away))
            def _():
                pltpu.make_async_copy(fbuf.at[s], dst, f_recv.at[0]).start()

    def stage_a(s):
        a, b, p = blocks(s)
        if s < PIECES:
            d_arrival(p).wait_recv()
        else:
            y_arrival(p).wait_recv()
            e_copy(p).start()
            e_arrival(p).wait_recv()
        if s == 0:
            w_load.wait()
        if s >= SLOTS:
            z1_copy(s - SLOTS).wait_send()
            z2_copy(s - SLOTS).wait_send()
        slot = s % SLOTS
        pbuf[slot] = jnp.zeros(pbuf.shape[1:], jnp.float32)

        @pl.loop(0, nb // kc)
        def _(i):
            cols = pl.ds(pl.multiple_of(i * kc, kc), kc)
            lhs = jnp.concatenate([dyf[rows(a, p), cols], dyf[rows(b, p), cols]], axis=0)
            pbuf[slot] += lax.dot_general(
                lhs, wv[:, cols], (((1,), (1,)), ((), ())), preferred_element_type=jnp.float32
            )

        z1_copy(s).start()

    def stage_b(s):
        z1_copy(s).wait_recv()
        slot = s % SLOTS
        pbuf[slot, kept(1 - zh)] += rb1[s, part(1 - zh)]
        z2_copy(s).start()

    def stage_c(s):
        z2_copy(s).wait_recv()
        total = (pbuf[s % SLOTS, kept(zh)] + rb1[s, part(zh)]) + rb2[s]
        fbuf[s] = total.astype(fbuf.dtype)
        f_start(s, True)

    def o_copy(j, slot):
        cols = pl.ds(pl.multiple_of(j * nc, nc), nc)
        return pltpu.make_async_copy(obuf.at[slot], dw_ref.at[:, cols], o_sem.at[slot])

    def dw_chunks(lo, hi):
        @pl.loop(lo, hi)
        def _(j):
            slot = j % 2

            @pl.when(j >= 2)
            def _():
                o_copy(j - 2, slot).wait()

            cols = pl.ds(pl.multiple_of(j * nc, nc), nc)
            obuf[slot] = lax.dot_general(
                xf[...], dyf[:, cols], (((0,), (0,)), ((), ())), preferred_element_type=jnp.float32
            )
            o_copy(j, slot).start()

    stage_a(0)
    stage_a(1)
    x_point(0)
    stage_b(0)
    stage_a(2)
    x_point(1)
    stage_b(1)
    stage_c(0)
    stage_a(3)
    x_point(2)
    stage_b(2)
    stage_c(1)
    stage_b(3)
    stage_c(2)
    x_point(3)
    stage_c(3)
    for s in range(PIECES, STEPS - 1):
        stage_a(s)
        x_point(s)
        stage_b(s)
        stage_c(s)
    last = STEPS - 1
    chunks = nb // nc
    stage_a(last)
    cut1, cut2 = (chunks * 5) // 14, (chunks * 10) // 14
    dw_chunks(0, cut1)
    stage_b(last)
    dw_chunks(cut1, cut2)
    stage_c(last)
    dw_chunks(cut2, chunks)

    for j in (chunks - 2, chunks - 1):
        o_copy(j, j % 2).wait()
    for p in range(PIECES):
        y_copy(p).wait_send()
        d_copy(p).wait_send()
        e_copy(p).wait_send()
    for s in range(STEPS - SLOTS, STEPS):
        z1_copy(s).wait_send()
        z2_copy(s).wait_send()
    for s in range(STEPS):
        f_start(s, False)
    for t in range(4):
        @pl.when(go_right)
        def _():
            x_right_copy(t).wait_send()

        @pl.when(go_left)
        def _():
            x_left_copy(t).wait_send()

    @pl.when(r != z)
    def _():
        x_out.wait_send()

    pltpu.make_async_copy(dx_ref, dx_ref, f_recv.at[0]).wait()


def solution(mesh):
    rows = P(("data", "r"), "c")

    def local(x, w, dy):
        tb, kb = x.shape
        nb = dy.shape[1]
        pr = tb // PIECES
        nc = pick(nb, 512)
        any_spec = pl.BlockSpec(memory_space=pl.ANY)
        dma = pltpu.SemaphoreType.DMA
        return pl.pallas_call(
            kernel,
            name="linear_backward",
            out_shape=(
                jax.ShapeDtypeStruct((tb, kb), jnp.bfloat16),
                jax.ShapeDtypeStruct((kb, nb), jnp.float32),
            ),
            in_specs=[any_spec] * 3,
            out_specs=(any_spec, any_spec),
            scratch_shapes=[
                pltpu.VMEM((4 * tb, nb), jnp.bfloat16),
                pltpu.VMEM((kb, nb), jnp.bfloat16),
                pltpu.VMEM((4 * tb, kb), jnp.bfloat16),
                pltpu.VMEM((SLOTS, 2 * pr, kb), jnp.float32),
                pltpu.VMEM((STEPS, pr, kb), jnp.float32),
                pltpu.VMEM((STEPS, pr // 2, kb), jnp.float32),
                pltpu.VMEM((STEPS, pr // 2, kb), jnp.bfloat16),
                pltpu.VMEM((2, kb, nc), jnp.float32),
                dma((PIECES,)), dma,
                dma((PIECES,)), dma((PIECES,)), dma((PIECES,)), dma((PIECES,)), dma((PIECES,)), dma((PIECES,)),
                dma((STEPS,)), dma((STEPS,)), dma((STEPS,)), dma((STEPS,)), dma((STEPS,)), dma((1,)),
                dma((1,)), dma((4,)), dma((4,)), dma((4,)), dma((2,)),
            ],
            compiler_params=pltpu.CompilerParams(
                collective_id=0, has_side_effects=True, vmem_limit_bytes=67_000_000
            ),
        )(x, w, dy)

    return jax.shard_map(local, mesh=mesh, in_specs=(rows, P("r", "c"), rows), out_specs=(rows, rows), check_vma=False)
```

time: 1190 us -> 279 us (0.23)
  the two profiles are of different devices: /device:TPU:0 before, /device:TPU:5 now
where the time goes in v2:
time: 279 us
  Pallas kernels  258 us (92%)
  local copies, waits for them, and re-layouts  19.8 us (7%)
    pallas_call x1, Pallas kernels, local(): pl.pallas_call(kernel, name='linear_backward', out_shape=(jax.ShapeDtypeS...  258 us
    unnamed x2, local copies, waits for them, and re-layouts  19.8 us

profile of v2, /device:TPU:5, one launch (start us, length us, event | category | flops | bytes accessed | tf_op | source)
XLA Modules:
  0.0 278.7 jit_solution(5510366843823303197)
XLA Ops:
  0.6 258.3 %linear_backward.1 = (bf16[512,896]{1,0:T(8,128)(2,1)}, f32[896,7168]{1,0:T(8,128)}) custom-call(bf16[512,896]{1,0:T(8,128)(2,1)} %x_ref.1, bf16[896,7168]{1,0:T(8,128)(2,1)} %w_ref.1, bf16[512,7168]{1,0:T(8,128)(2,1)} %dy_ref.1), custom_call_target="tpu_custom_call" | custom-call | tf_op jit(solution)/shard_map/linear_backward/pallas_call | solution.py:285
  259.0 2.2 copy.7
  261.1 17.6 %copy.8 = f32[896,7168]{1,0:T(8,128)} copy(f32[896,7168]{1,0:T(8,128)} %get-tuple-element.5) | data formatting | bytes 51380224

commit v3 on v2

v3 whole, which is shorter than its diff:
```python
import jax
import jax.numpy as jnp
from jax import lax
from jax.experimental import pallas as pl
from jax.experimental.pallas import tpu as pltpu
from jax.sharding import PartitionSpec as P

MESH = pl.DeviceIdType.MESH
NEAR = ((0, 2), (2, 2), (4, 2), (6, 2))
FAR = ((0, 2), (2, 2), (4, 2), (6, 1), (7, 1))
LATE = 6
STEPS = len(NEAR) + len(FAR)
SLOTS = 4


def pick(size, want):
    return want if size % want == 0 else 128


def kernel(
    x_ref, w_ref, dy_ref, dx_ref, dw_ref, xl_ref, dyl_ref,
    dyf, wv, xf, xmid, pbuf, rb1, rb2, fbuf, obuf,
    ld_sem, w_sem, y_send, y_recv, d_send, d_recv, e_send, e_recv,
    z1_send, z1_recv, z2_send, z2_recv, f_send, f_recv,
    x_src, x_recv, x_left, x_right, m_sem, o_sem, l_sem,
):
    z, r = lax.axis_index("c"), lax.axis_index("r")
    y, k = r // 2, r % 2
    mate, over, over_mate = 2 * y + 1 - k, 2 * (1 - y) + k, 2 * (1 - y) + 1 - k
    zb, zh = z % 2, z // 2
    z1, z2 = 2 * zh + 1 - zb, 2 * (1 - zh) + zb
    tb, kb = x_ref.shape
    nb = dy_ref.shape[1]
    unit = tb // 8
    kc, nc = pick(nb, 1024), pick(nb, 512)

    def rows(block, span):
        return pl.ds(pl.multiple_of(block * tb + span[0] * unit, unit), span[1] * unit)

    def send(src, dst, ssem, rsem, c=None, rr=None):
        dev = {}
        if c is not None:
            dev["c"] = c
        if rr is not None:
            dev["r"] = rr
        return pltpu.make_async_remote_copy(
            src_ref=src, dst_ref=dst, send_sem=ssem, recv_sem=rsem, device_id=dev, device_id_type=MESH
        )

    def load(p):
        src = dy_ref.at[pl.ds(NEAR[p][0] * unit, NEAR[p][1] * unit)]
        return pltpu.make_async_copy(src, dyf.at[rows(r, NEAR[p])], ld_sem.at[p])

    w_load = pltpu.make_async_copy(w_ref, wv, w_sem)
    for p in range(len(NEAR)):
        load(p).start()
    w_load.start()

    barrier = pltpu.get_barrier_semaphore()
    for i in range(1, 16):
        peer = {"c": (z + i // 4) % 4, "r": (r + i % 4) % 4}
        pl.semaphore_signal(barrier, inc=1, device_id=peer, device_id_type=MESH)
    pl.semaphore_wait(barrier, 15)

    def xrows(t):
        return pl.ds(pl.multiple_of(t * tb, tb), tb)

    detour = jnp.logical_and(k == 1, y != zh)
    relay = jnp.logical_and(k == 1, y == zh)
    direct = jnp.logical_and(jnp.logical_not(detour), r != z)
    x_own = pltpu.make_async_copy(x_ref, xf.at[xrows(r)], x_recv.at[r])
    x_out = send(x_ref, xf.at[xrows(r)], x_src.at[0], x_recv.at[r], c=z, rr=z)
    m_out = send(x_ref, xmid, m_sem.at[0], m_sem.at[1], c=z2)
    m_pass = send(xmid, xf.at[xrows(r)], m_sem.at[2], x_recv.at[r], c=z, rr=z2)

    @pl.when(r == z)
    def _():
        x_own.start()

    @pl.when(direct)
    def _():
        x_out.start()

    @pl.when(detour)
    def _():
        m_out.start()

    def y_copy(p):
        return send(dyf.at[rows(r, FAR[p])], dyf.at[rows(r, FAR[p])], y_send.at[p], y_recv.at[p], rr=over)

    def d_copy(p):
        return send(dyf.at[rows(r, NEAR[p])], dyf.at[rows(r, NEAR[p])], d_send.at[p], d_recv.at[p], rr=mate)

    def e_copy(p):
        return send(dyf.at[rows(over, FAR[p])], dyf.at[rows(over, FAR[p])], e_send.at[p], e_recv.at[p], rr=mate)

    def y_arrival(p):
        return send(dyf.at[rows(over, FAR[p])], dyf.at[rows(over, FAR[p])], y_send.at[p], y_recv.at[p], rr=over)

    def d_arrival(p):
        return send(dyf.at[rows(mate, NEAR[p])], dyf.at[rows(mate, NEAR[p])], d_send.at[p], d_recv.at[p], rr=mate)

    def e_arrival(p):
        at = rows(over_mate, FAR[p])
        return send(dyf.at[at], dyf.at[at], e_send.at[p], e_recv.at[p], rr=mate)

    for p in range(len(NEAR)):
        load(p).wait()
        if p == 0:
            y_copy(0).start()
        d_copy(p).start()

    def y_rest():
        @pl.when(relay)
        def _():
            m_out.wait_recv()
            m_pass.start()

        for p in range(1, len(FAR)):
            y_copy(p).start()

    def x_route(t):
        near = y == t // 2
        head = jnp.where(jnp.logical_or(near, t % 2 == 0), r, (r + 2) % 4)
        hops = jnp.where(z >= head, z - head, head - z)
        turn = jnp.where(near, t % 2, 2 + t % 2)
        go_right = jnp.logical_and(z >= head, z < 3)
        go_left = jnp.logical_and(z <= head, z > 0)
        return turn + hops, go_right, go_left

    routes = [x_route(t) for t in range(4)]

    def x_right_copy(t):
        return send(xf.at[xrows(t)], xf.at[xrows(t)], x_right.at[t], x_recv.at[t], c=z + 1)

    def x_left_copy(t):
        return send(xf.at[xrows(t)], xf.at[xrows(t)], x_left.at[t], x_recv.at[t], c=z - 1)

    def x_point(j):
        for t in range(4):
            when, go_right, go_left = routes[t]
            live = when == j

            @pl.when(live)
            def _():
                pltpu.make_async_copy(x_ref, xf.at[xrows(t)], x_recv.at[t]).wait()

            @pl.when(jnp.logical_and(live, go_right))
            def _():
                x_right_copy(t).start()

            @pl.when(jnp.logical_and(live, go_left))
            def _():
                x_left_copy(t).start()

    def blocks(s):
        return (r, mate, NEAR[s]) if s < len(NEAR) else (over, over_mate, FAR[s - len(NEAR)])

    def size(s):
        return blocks(s)[2][1] * unit

    def z1_copy(s):
        n = size(s)
        half = pl.ds(pl.multiple_of((1 - zb) * n, n), n)
        return send(pbuf.at[s % SLOTS, half], rb1.at[s, pl.ds(0, n)], z1_send.at[s], z1_recv.at[s], c=z1)

    def kept(s, i):
        n = size(s) // 2
        return pl.ds(pl.multiple_of(zb * 2 * n + i * n, n), n)

    def part(s, i):
        n = size(s) // 2
        return pl.ds(pl.multiple_of(i * n, n), n)

    def z2_copy(s):
        dst = rb2.at[s, pl.ds(0, size(s) // 2)]
        return send(pbuf.at[s % SLOTS, kept(s, 1 - zh)], dst, z2_send.at[s], z2_recv.at[s], c=z2)

    def f_start(s, begin):
        a, b, span = blocks(s)
        n = size(s) // 2
        owner = a + zb * (b - a)
        src = fbuf.at[s, pl.ds(0, n)]
        dst = dx_ref.at[pl.ds(pl.multiple_of(span[0] * unit + zh * n, n), n)]
        away = jnp.logical_or(z != r, owner != r)

        @pl.when(away)
        def _():
            copy = send(src, dst, f_send.at[s], f_recv.at[0], c=r, rr=owner)
            copy.start() if begin else copy.wait_send()

        if begin:

            @pl.when(jnp.logical_not(away))
            def _():
                pltpu.make_async_copy(src, dst, f_recv.at[0]).start()

    def stage_a(s):
        a, b, span = blocks(s)
        p = s - len(NEAR)
        if p < 0:
            d_arrival(s).wait_recv()
        else:
            y_arrival(p).wait_recv()
            e_copy(p).start()
            e_arrival(p).wait_recv()
        if s == 0:
            w_load.wait()
        if s >= SLOTS:
            z1_copy(s - SLOTS).wait_send()
            z2_copy(s - SLOTS).wait_send()
        slot, n = s % SLOTS, 2 * size(s)
        pbuf[slot, :n] = jnp.zeros((n, kb), jnp.float32)

        @pl.loop(0, nb // kc)
        def _(i):
            cols = pl.ds(pl.multiple_of(i * kc, kc), kc)
            lhs = jnp.concatenate([dyf[rows(a, span), cols], dyf[rows(b, span), cols]], axis=0)
            pbuf[slot, :n] += lax.dot_general(
                lhs, wv[:, cols], (((1,), (1,)), ((), ())), preferred_element_type=jnp.float32
            )

        z1_copy(s).start()

    def stage_b(s):
        z1_copy(s).wait_recv()
        pbuf[s % SLOTS, kept(s, 1 - zh)] += rb1[s, part(s, 1 - zh)]
        z2_copy(s).start()

    def stage_c(s):
        z2_copy(s).wait_recv()
        n = size(s) // 2
        total = (pbuf[s % SLOTS, kept(s, zh)] + rb1[s, part(s, zh)]) + rb2[s, :n]
        fbuf[s, :n] = total.astype(fbuf.dtype)
        f_start(s, True)

    def o_copy(j, slot):
        cols = pl.ds(pl.multiple_of(j * nc, nc), nc)
        return pltpu.make_async_copy(obuf.at[slot], dw_ref.at[:, cols], o_sem.at[slot])

    early = [pl.ds(pl.multiple_of(y * 2 * tb, 2 * tb), 2 * tb), rows(2 * (1 - y), (0, LATE)), rows(3 - 2 * y, (0, LATE))]

    def dw_early():
        @pl.loop(0, nb // nc)
        def _(j):
            slot = j % 2

            @pl.when(j >= 2)
            def _():
                o_copy(j - 2, slot).wait()

            cols = pl.ds(pl.multiple_of(j * nc, nc), nc)
            terms = [
                lax.dot_general(xf[at], dyf[at, cols], (((0,), (0,)), ((), ())), preferred_element_type=jnp.float32)
                for at in early
            ]
            obuf[slot] = (terms[0] + terms[1]) + terms[2]
            o_copy(j, slot).start()

    late = (8 - LATE) * unit

    def x_late(i):
        src = xf.at[rows((over, over_mate)[i], (LATE, 8 - LATE))]
        return pltpu.make_async_copy(src, xl_ref.at[pl.ds(i * late, late)], l_sem.at[i])

    def dy_late(i):
        src = dyf.at[rows((over, over_mate)[i], (LATE, 8 - LATE))]
        return pltpu.make_async_copy(src, dyl_ref.at[pl.ds(i * late, late)], l_sem.at[2 + i])

    stage_a(0)
    stage_a(1)
    y_rest()
    x_point(0)
    stage_b(0)
    stage_a(2)
    x_point(1)
    stage_b(1)
    stage_c(0)
    stage_a(3)
    x_point(2)
    stage_b(2)
    stage_c(1)
    stage_b(3)
    stage_c(2)
    stage_c(3)
    stage_a(4)
    x_point(3)
    stage_b(4)
    stage_c(4)
    x_point(4)
    stage_a(5)
    x_point(5)
    stage_b(5)
    stage_c(5)
    x_point(6)
    x_late(0).start()
    x_late(1).start()
    stage_a(6)
    stage_b(6)
    stage_c(6)
    dw_early()
    stage_a(7)
    stage_b(7)
    stage_c(7)
    stage_a(8)
    dy_late(0).start()
    dy_late(1).start()
    stage_b(8)
    stage_c(8)

    chunks = nb // nc
    for j in (chunks - 2, chunks - 1):
        o_copy(j, j % 2).wait()
    for p in range(len(NEAR)):
        d_copy(p).wait_send()
    for p in range(len(FAR)):
        y_copy(p).wait_send()
        e_copy(p).wait_send()
    for s in range(STEPS - SLOTS, STEPS):
        z1_copy(s).wait_send()
        z2_copy(s).wait_send()
    for s in range(STEPS):
        f_start(s, False)
    for t in range(4):
        _, go_right, go_left = routes[t]

        @pl.when(go_right)
        def _():
            x_right_copy(t).wait_send()

        @pl.when(go_left)
        def _():
            x_left_copy(t).wait_send()

    @pl.when(direct)
    def _():
        x_out.wait_send()

    @pl.when(detour)
    def _():
        m_out.wait_send()

    @pl.when(relay)
    def _():
        m_pass.wait_send()

    for i in range(2):
        x_late(i).wait()
        dy_late(i).wait()
    pltpu.make_async_copy(dx_ref, dx_ref, f_recv.at[0]).wait()


def solution(mesh):
    rows = P(("data", "r"), "c")

    def local(x, w, dy):
        tb, kb = x.shape
        nb = dy.shape[1]
        pr, late = tb // 4, 2 * tb * (8 - LATE) // 8
        nc = pick(nb, 512)
        any_spec = pl.BlockSpec(memory_space=pl.ANY)
        dma = pltpu.SemaphoreType.DMA
        far, steps = (len(FAR),), (STEPS,)
        dx, dw_early, x_late, dy_late = pl.pallas_call(
            kernel,
            name="linear_backward",
            out_shape=(
                jax.ShapeDtypeStruct((tb, kb), jnp.bfloat16),
                jax.ShapeDtypeStruct((kb, nb), jnp.float32),
                jax.ShapeDtypeStruct((late, kb), jnp.bfloat16),
                jax.ShapeDtypeStruct((late, nb), jnp.bfloat16),
            ),
            in_specs=[any_spec] * 3,
            out_specs=(any_spec,) * 4,
            scratch_shapes=[
                pltpu.VMEM((4 * tb, nb), jnp.bfloat16),
                pltpu.VMEM((kb, nb), jnp.bfloat16),
                pltpu.VMEM((4 * tb, kb), jnp.bfloat16),
                pltpu.VMEM((tb, kb), jnp.bfloat16),
                pltpu.VMEM((SLOTS, 2 * pr, kb), jnp.float32),
                pltpu.VMEM((STEPS, pr, kb), jnp.float32),
                pltpu.VMEM((STEPS, pr // 2, kb), jnp.float32),
                pltpu.VMEM((STEPS, pr // 2, kb), jnp.bfloat16),
                pltpu.VMEM((2, kb, nc), jnp.float32),
                dma((len(NEAR),)), dma, dma(far), dma(far), dma((len(NEAR),)), dma((len(NEAR),)), dma(far), dma(far),
                dma(steps), dma(steps), dma(steps), dma(steps), dma(steps), dma((1,)),
                dma((1,)), dma((4,)), dma((4,)), dma((4,)), dma((3,)), dma((2,)), dma((4,)),
            ],
            compiler_params=pltpu.CompilerParams(
                collective_id=0, has_side_effects=True, vmem_limit_bytes=67_000_000
            ),
        )(x, w, dy)
        dw_late = lax.dot_general(x_late, dy_late, (((0,), (0,)), ((), ())), preferred_element_type=jnp.float32)
        return dx, dw_early + dw_late

    return jax.shard_map(local, mesh=mesh, in_specs=(rows, P("r", "c"), rows), out_specs=(rows, rows), check_vma=False)
```

time: 279 us -> 346 us (1.24)
  the two profiles are of different devices: /device:TPU:5 before, /device:TPU:19 now
where the time goes in v3:
time: 346 us
  Pallas kernels  322 us (93%)
  matrix products  22.3 us (6%)
    pallas_call x1, Pallas kernels, local(): pl.pallas_call(kernel, name='linear_backward', out_shape=(jax.ShapeDtypeS...  322 us
    dot_general x1, matrix products, local(): lax.dot_general(x_late, dy_late, (((0,), (0,)), ((), ())), preferred_elem...  22.3 us

profile of v3, /device:TPU:19, one launch (start us, length us, event | category | flops | bytes accessed | tf_op | source)
XLA Modules:
  0.0 345.6 jit_solution(806641916911633324)
XLA Ops:
  0.6 321.8 %linear_backward.1 = (bf16[512,896]{1,0:T(8,128)(2,1)}, f32[896,7168]{1,0:T(8,128)}, bf16[256,896]{1,0:T(8,128)(2,1)}, bf16[256,7168]{1,0:T(8,128)(2,1)}) custom-call(bf16[512,896]{1,0:T(8,128)(2,1)} %x_ref.1, bf16[896,7168]{1,0:T(8,128)(2,1)} %w_ref.1, bf16[512,7168]{1,0:T(8,128)(2,1)} %dy_ref.1), custom_call_target="tpu_custom_call" | custom-call | tf_op jit(solution)/shard_map/linear_backward/pallas_call | solution.py:364
  322.4 0.0 copy-start
  322.4 22.3 %convolution_add_fusion = f32[896,7168]{1,0:T(8,128)} fusion(f32[896,7168]{1,0:T(8,128)} %get-tuple-element.7, bf16[256,896]{1,0:T(8,128)(2,1)} %get-tuple-element.8, bf16[256,7168]{1,0:T(8,128)(2,1)} %get-tuple-element.9), kind=kOutput, calls=%fused_computation | convolution fusion | flops 3294756864 | bytes 55508992 | tf_op jit(solution)/shard_map/dot_general | solution.py:393
  344.7 0.0 copy-done
  344.7 0.9 copy.6
Async XLA Ops:
  322.4 22.3 %copy-start = (bf16[512,896]{1,0:T(8,128)(2,1)S(1)}, bf16[512,896]{1,0:T(8,128)(2,1)}, u32[]{:S(2)}) copy-start(bf16[512,896]{1,0:T(8,128)(2,1)} %get-tuple-element.12) | copy-start | bytes 2752516
